TPU v7x, 256 devices: a whole 4x4x8 slice. The times are simulated.
256 devices in a mesh: pop: 8 (over x_lo, y), dp: 32 (over z, x_hi, core).
Axes of the slice: x: 4 (x_hi: 2, x_lo: 2; x = x_hi * 2 + x_lo), y: 4, z: 8, core: 2. Of those that a mesh axis runs over, the one named last changes fastest.
Arguments:
- observations: bfloat16 [8, 16384, 256], P('pop', 'dp'), may hold values from -6 to 6
- returns: float32 [8, 16384], P('pop', 'dp'), may hold values from 0 to 2
- actions: int32 [8, 16384], P('pop', 'dp'), may hold values from 0 to 17
- w_input: bfloat16 [8, 256, 2048], P('pop', 'dp'), may hold values from -0.375 to 0.375
- w_middle: bfloat16 [8, 2048, 2048], P('pop', 'dp'), may hold values from -0.125 to 0.125
- w_head: bfloat16 [8, 2048, 18], P('pop', 'dp'), may hold values from -0.125 to 0.125
- log_rate: float32 [8], replicated, may hold values from 3 to 4
- copy_from: int32 [8], replicated, may hold values from 0 to 1, as said below
- perturb: int32 [8], replicated, may hold values from 0 to 2
Outputs:
- next_input: bfloat16 [8, 256, 2048], P('pop', 'dp')
- next_middle: bfloat16 [8, 2048, 2048], P('pop', 'dp')
- next_head: bfloat16 [8, 2048, 18], P('pop', 'dp')
- next_log_rate: float32 [8], P('pop')
- fitness: float32 [8], P('pop')
Inputs may be any that keep to these rules, and one draw needn't show every extreme that they name: Some two members that lie 4 apart have copy_from 1.
All inputs are finite; a program needn't handle non-finite values.
Results may differ from a plain program's by a relative error of at most 0.014.
Values may be sent and summed in bfloat16 or wider, within the bound.
A program may use at most 128 MiB of HBM per device.

v0:
```python
import jax
import jax.numpy as jnp
from jax import lax
from jax.sharding import PartitionSpec as P

CAP = 2.0


def joined_along(parts, dim):
    parts = jnp.moveaxis(parts, 0, dim)
    lengths = parts.shape
    return parts.reshape(*lengths[:dim], lengths[dim] * lengths[dim + 1], *lengths[dim + 2 :])


def gather_packed(arrays, axis, dims):
    line = jnp.concatenate([a.reshape(-1) for a in arrays])
    lines, at, done = (lax.all_gather(line, axis), 0, [])
    for a, dim in zip(arrays, dims):
        parts = lines[:, at : at + a.size].reshape(-1, *a.shape)
        done.append(joined_along(parts, dim))
        at += a.size
    return tuple(done)


def from_everyone(shard, axis):
    peers = lax.axis_size(axis)
    return lax.all_to_all(
        jnp.broadcast_to(shard[None], (peers, *shard.shape)), axis, 0, 0, tiled=True
    )


def of_everyone(shard, axis):
    everything = from_everyone(shard, axis)
    return jnp.sum(everything, axis=0)


def in_blocks(shard, dim, peers):
    before, after = (shard.shape[:dim], shard.shape[dim + 1 :])
    return jnp.moveaxis(shard.reshape(*before, peers, -1, *after), dim, 0)


def sum_at_owner(shard, axis, dim):
    peers = lax.axis_size(axis)
    parts = lax.all_to_all(in_blocks(shard, dim, peers), axis, 0, 0, tiled=True)
    return jnp.sum(parts.astype(jnp.float32), axis=0)


def shifted(block, axis, distance):
    devices = range(lax.axis_size(axis))
    route = [((i - distance) % len(devices), i) for i in devices]
    return lax.ppermute(block, axis, route)


def silu_slope(pre):
    sig = jax.nn.sigmoid(pre)
    return sig * (1.0 + pre * (1.0 - sig))


def contract_rows(left, right):
    return lax.dot_general(
        left, right, (((0,), (0,)), ((), ())), preferred_element_type=jnp.float32
    )


def contract_cols(left, right):
    return lax.dot_general(
        left, right, (((1,), (1,)), ((), ())), preferred_element_type=jnp.float32
    )


def local(observations, returns, actions, w_input, w_middle, w_head, log_rate, copy_from, perturb):
    obs = observations[0]
    gains = returns[0]
    chosen = actions[0]
    own_first = w_input[0]
    own_middle = w_middle[0]
    own_head = w_head[0]
    rows = obs.shape[0]
    batch = rows * lax.axis_size("dp")
    first, head = gather_packed((own_first, own_head), "dp", (0, 0))
    pre1 = jnp.dot(obs, first, preferred_element_type=jnp.float32)
    hidden1 = jax.nn.silu(pre1).astype(jnp.bfloat16)
    whole = lax.all_gather(own_middle, "dp", axis=0, tiled=True)
    pre2 = jnp.dot(hidden1, whole, preferred_element_type=jnp.float32)
    hidden2 = jax.nn.silu(pre2).astype(jnp.bfloat16)
    squash = jnp.tanh(jnp.dot(hidden2, head, preferred_element_type=jnp.float32) / CAP)
    logits = CAP * squash
    logp = logits - jnp.log(jnp.sum(jnp.exp(logits), axis=1, keepdims=True))
    onehot = (chosen[:, None] == lax.broadcasted_iota(jnp.int32, logits.shape, 1)).astype(
        jnp.float32
    )
    taken = jnp.sum(logp * onehot, axis=1)
    fitness = of_everyone(jnp.sum(gains * taken) / batch, "dp")
    grad_raw = (
        -(gains / batch)[:, None] * (onehot - jnp.exp(logp)) * (1.0 - squash * squash)
    ).astype(jnp.bfloat16)
    head_term = contract_rows(hidden2, grad_raw)
    grad_pre2 = (contract_cols(grad_raw, head) * silu_slope(pre2)).astype(jnp.bfloat16)
    grad_middle = lax.psum_scatter(
        contract_rows(hidden1, grad_pre2).astype(jnp.bfloat16),
        "dp",
        scatter_dimension=0,
        tiled=True,
    ).astype(jnp.float32)
    member = lax.axis_index("pop")
    members = lax.axis_size("pop")
    rate = jnp.exp(lax.dynamic_index_in_dim(log_rate, member, keepdims=False))
    new_middle = (own_middle.astype(jnp.float32) - rate * grad_middle).astype(jnp.bfloat16)
    back = contract_cols(grad_pre2, whole)
    grad_pre1 = (back * silu_slope(pre1)).astype(jnp.bfloat16)
    input_term = contract_rows(obs, grad_pre1)
    grad_first, grad_head = (
        sum_at_owner(input_term.astype(jnp.bfloat16), "dp", 0),
        sum_at_owner(head_term.astype(jnp.bfloat16), "dp", 0),
    )
    new_first = (own_first.astype(jnp.float32) - rate * grad_first).astype(jnp.bfloat16)
    new_head = (own_head.astype(jnp.float32) - rate * grad_head).astype(jnp.bfloat16)
    moved_first, moved_middle, moved_head = shifted((new_first, new_middle, new_head), "pop", 1)
    flag = lax.dynamic_index_in_dim(copy_from, member, keepdims=False) == 1
    out_first = jnp.where(flag, moved_first, new_first)
    out_middle = jnp.where(flag, moved_middle, new_middle)
    out_head = jnp.where(flag, moved_head, new_head)
    source = jnp.where(flag, (member + members - 1) % members, member)
    pick = lax.dynamic_index_in_dim(perturb, member, keepdims=False)
    offset = jnp.where(pick == 0, -0.2, jnp.where(pick == 1, 0.0, 0.2)).astype(jnp.float32)
    next_rate = lax.dynamic_index_in_dim(log_rate, source, keepdims=False) + offset
    return (
        out_first[None],
        out_middle[None],
        out_head[None],
        next_rate.reshape(1),
        fitness.reshape(1),
    )


def solution(mesh):
    in_specs = (
        P("pop", "dp", None),
        P("pop", "dp"),
        P("pop", "dp"),
        P("pop", "dp", None),
        P("pop", "dp", None),
        P("pop", "dp", None),
        P(),
        P(),
        P(),
    )
    out_specs = (
        P("pop", "dp", None),
        P("pop", "dp", None),
        P("pop", "dp", None),
        P("pop"),
        P("pop"),
    )
    return jax.shard_map(local, mesh=mesh, in_specs=in_specs, out_specs=out_specs, check_vma=False)
```

profile of v0, /device:TPU:2, one launch (start us, length us, event | category | flops | bytes accessed | tf_op | source)
XLA Modules:
  0.0 389.5 jit_solution(15649825401868657893)
XLA Ops:
  7.2 0.0 copy-start
  7.2 0.0 all-gather.8.cloned.1.call-start
  7.2 0.8 copy.37
  8.1 0.1 reshape_squeeze.7
  8.2 0.8 copy.50
  9.0 0.7 reshape.61
  9.7 0.0 all-gather.8.cloned.1.call-update
  9.7 0.0 all-gather.6.cloned.1.call-start
  9.7 0.7 all-gather.6.cloned.1.call-update
  10.4 0.0 reduce-scatter.2.cloned.1.call-start
  10.5 83.0 %all-gather.8.cloned.1.call-done = bf16[32,1,17536]{2,1,0:T(2,128)(2,1)} async-done(((bf16[1,1,17536]{2,1,0:T(2,128)(2,1)}), bf16[32,1,17536]{2,1,0:T(2,128)(2,1)}) %all-gather.8.cloned.1.call-update) | async-done | bytes 1122320 | tf_op jit(solution)/shard_map/all_gather | solution.py:17
  93.5 1.8 copy.53
  95.3 0.1 slice.8
  95.3 0.5 reshape_reshape.6
  95.9 1.2 reshape_reshape.7
  97.1 0.0 copy-done
  97.1 2.7 fusion.20
  99.8 94.4 %all-gather.6.cloned.1.call-done = bf16[1,2048,2048]{2,1,0:T(8,128)(2,1)} async-done(((bf16[1,64,2048]{2,1,0:T(8,128)(2,1)}), bf16[1,2048,2048]{2,1,0:T(8,128)(2,1)}) %all-gather.6.cloned.1.call-update) | async-done | bytes 8388624 | tf_op jit(solution)/shard_map/all_gather | solution.py:83
  194.3 9.0 %multiply_convert_fusion.1 = (bf16[512,2048]{0,1:T(8,128)(2,1)S(1)}, f32[512,2048]{0,1:T(8,128)S(1)}) fusion(bf16[1,2048,2048]{2,1,0:T(8,128)(2,1)} %all-gather.6.cloned.1.call-done, f32[2048,512]{1,0:T(8,128)} %fusion.20), kind=kOutput, calls=%fused_computation.17 | convolution fusion | flops 4305453056 | bytes 18874368 | tf_op jit(solution)/shard_map/dot_general | solution.py:84
  203.3 0.5 exponential_reduce_fusion
  203.7 0.0 copy-done.5
  203.8 0.6 multiply_reduce_fusion
  204.4 1.7 multiply_convert_fusion
  206.1 1.3 copy-done.10
  207.4 6.9 %convolution_convert_fusion = bf16[2048,2048]{1,0:T(8,128)(2,1)} fusion(bf16[512,2048]{0,1:T(8,128)(2,1)S(1)} %multiply_convert_fusion, f32[2048,512]{1,0:T(8,128)S(1)} %copy-done.1), kind=kOutput, calls=%fused_computation.4 | convolution fusion | flops 4304404480 | bytes 14680064 | tf_op jit(solution)/shard_map/dot_general | solution.py:60
  214.3 0.0 reduce-scatter.2.cloned.1.call-update
  215.0 0.6 broadcast_in_dim.20
  215.6 5.5 %all-to-all-start.2 = ((f32[32,1,1]{2,1,0:T(1,128)}), f32[32,1,1]{2,1,0:T(1,128)S(1)}, u32[]{:S(2)}, u32[]{:S(2)}) async-start(f32[32,1,1]{2,1,0:T(1,128)} %broadcast_in_dim.20), calls=%async_computation.3 | async-start | bytes 32768 | tf_op jit(solution)/shard_map/all_to_all | solution.py:27
  221.1 0.6 convolution_convert_fusion.2
  221.8 0.2 reshape.54
  222.0 0.1 copy.54
  222.1 0.8 reshape.64
  222.8 8.0 %all-to-all-done.2 = f32[32,1,1]{2,1,0:T(1,128)S(1)} async-done(((f32[32,1,1]{2,1,0:T(1,128)}), f32[32,1,1]{2,1,0:T(1,128)S(1)}, u32[]{:S(2)}, u32[]{:S(2)}) %all-to-all-start.2) | async-done | bytes 160 | tf_op jit(solution)/shard_map/all_to_all | solution.py:27
  230.8 4.0 %all-to-all-start.1 = ((bf16[32,2,576]{2,1,0:T(2,128)(2,1)}), bf16[32,2,576]{2,1,0:T(2,128)(2,1)S(1)}, u32[]{:S(2)}, u32[]{:S(2)}) async-start(bf16[32,2,576]{2,1,0:T(2,128)(2,1)} %reshape.64), calls=%async_computation.2 | async-start | bytes 163840 | tf_op jit(solution)/shard_map/all_to_all | solution.py:44
  234.9 0.0 copy-start.8
  234.9 0.0 copy-start.6
  234.9 0.0 copy-start.4
  234.9 0.0 copy-start.9
  234.9 0.0 copy-start.3
  234.9 0.0 copy-start.2
  234.9 12.9 %fusion.14 = bf16[32,8,2048]{2,1,0:T(8,128)(2,1)} fusion(f32[2048,512]{1,0:T(8,128)} %fusion.20, bf16[512,2048]{0,1:T(8,128)(2,1)} %copy-done.10, bf16[1,2048,2048]{2,1,0:T(8,128)(2,1)} %all-gather.6.cloned.1.call-done, bf16[1,512,256]{2,1,0:T(8,128)(2,1)S(1)} %copy-done), kind=kOutput, calls=%fused_computation.20 | convolution fusion | flops 4841799680 | bytes 15990784 | tf_op jit(solution)/shard_map/dot_general | solution.py:60
  247.8 0.0 all-to-all-done.1
  247.8 9.6 %all-to-all-start = ((bf16[32,8,2048]{2,1,0:T(8,128)(2,1)}), bf16[32,8,2048]{2,1,0:T(8,128)(2,1)S(1)}, u32[]{:S(2)}, u32[]{:S(2)}) async-start(bf16[32,8,2048]{2,1,0:T(8,128)(2,1)} %fusion.14), calls=%async_computation | async-start | bytes 2097152 | tf_op jit(solution)/shard_map/all_to_all | solution.py:44
  257.5 0.6 dynamic_slice.14
  258.7 0.0 copy-done.6
  258.7 0.6 fusion.27
  260.0 0.2 reshape.65
  260.2 0.1 convert_reduce_fusion.1
  260.3 1.6 collective-permute-start.2
  261.8 0.0 copy-done.9
  261.8 0.6 dynamic_slice.17
  264.4 0.6 reduce_sum.59
  265.0 1.1 collective-permute-done.2
  266.1 0.6 select_bitcast_fusion.2
  266.7 25.0 %all-to-all-done = bf16[32,8,2048]{2,1,0:T(8,128)(2,1)S(1)} async-done(((bf16[32,8,2048]{2,1,0:T(8,128)(2,1)}), bf16[32,8,2048]{2,1,0:T(8,128)(2,1)S(1)}, u32[]{:S(2)}, u32[]{:S(2)}) %all-to-all-start) | async-done | bytes 1048608 | tf_op jit(solution)/shard_map/all_to_all | solution.py:44
  291.7 0.2 convert_reduce_fusion
  291.9 1.6 collective-permute-start
  293.4 78.0 %reduce-scatter.2.cloned.1.call-done = bf16[64,2048]{1,0:T(8,128)(2,1)} async-done(((bf16[2048,2048]{1,0:T(8,128)(2,1)}), bf16[64,2048]{1,0:T(8,128)(2,1)}) %reduce-scatter.2.cloned.1.call-update) | async-done | bytes 262160 | tf_op jit(solution)/shard_map/reduce_scatter | solution.py:99
  371.5 1.0 fusion.18
  372.5 1.5 collective-permute-start.1
  374.0 0.0 collective-permute-done
  374.0 0.6 select_bitcast_fusion.1
  374.6 6.5 %collective-permute-done.1 = bf16[64,2048]{1,0:T(8,128)(2,1)S(1)} collective-permute-done((bf16[64,2048]{1,0:T(8,128)(2,1)S(1)}, bf16[64,2048]{1,0:T(8,128)(2,1)S(1)}, u32[]{:S(2)}, u32[]{:S(2)}) %collective-permute-start.1) | collective-permute-done | bytes 262176 | tf_op jit(solution)/shard_map/ppermute | solution.py:51
  381.1 0.7 select_bitcast_fusion
  (16 shorter events, 0.1 us)
Async XLA Ops:
  7.2 90.0 %copy-start = (bf16[1,512,256]{2,1,0:T(8,128)(2,1)S(1)}, bf16[1,512,256]{2,1,0:T(8,128)(2,1)}, u32[]{:S(2)}) copy-start(bf16[1,512,256]{2,1,0:T(8,128)(2,1)} %param.9) | copy-start | bytes 786436
  7.2 86.3 %all-gather.8.cloned.1.call-start = ((), (), s32[]{:S(2)}) async-start(), calls=%async_computation.6 | async-start | bytes 2314752 | tf_op jit(solution)/shard_map/all_gather | solution.py:17
  9.7 184.6 %all-gather.6.cloned.1.call-start = ((), (), s32[]{:S(2)}) async-start(), calls=%async_computation.5 | async-start | bytes 8650752 | tf_op jit(solution)/shard_map/all_gather | solution.py:83
  10.4 361.1 %reduce-scatter.2.cloned.1.call-start = ((), (), s32[]{:S(2)}) async-start(), calls=%async_computation.4 | async-start | bytes 8650752 | tf_op jit(solution)/shard_map/reduce_scatter | solution.py:99
  99.8 103.9 %copy-start.5 = (s32[1,512]{1,0:T(1,128)S(1)}, s32[1,512]{1,0:T(1,128)}, u32[]{:S(2)}) copy-start(s32[1,512]{1,0:T(1,128)} %param.11) | copy-start | bytes 6148
  99.8 103.9 %copy-start.7 = (f32[1,512]{1,0:T(1,128)S(1)}, f32[1,512]{1,0:T(1,128)}, u32[]{:S(2)}) copy-start(f32[1,512]{1,0:T(1,128)} %param.10) | copy-start | bytes 6148
  204.4 3.0 copy-start.1
  206.1 1.3 copy-start.10
  215.6 15.2 %all-to-all-start.2 = ((f32[32,1,1]{2,1,0:T(1,128)}), f32[32,1,1]{2,1,0:T(1,128)S(1)}, u32[]{:S(2)}, u32[]{:S(2)}) async-start(f32[32,1,1]{2,1,0:T(1,128)} %broadcast_in_dim.20), calls=%async_computation.3 | async-start | bytes 32768 | tf_op jit(solution)/shard_map/all_to_all | solution.py:27
  230.8 17.0 %all-to-all-start.1 = ((bf16[32,2,576]{2,1,0:T(2,128)(2,1)}), bf16[32,2,576]{2,1,0:T(2,128)(2,1)S(1)}, u32[]{:S(2)}, u32[]{:S(2)}) async-start(bf16[32,2,576]{2,1,0:T(2,128)(2,1)} %reshape.64), calls=%async_computation.2 | async-start | bytes 163840 | tf_op jit(solution)/shard_map/all_to_all | solution.py:44
  234.9 22.6 %copy-start.8 = (s32[8]{0:T(128)S(1)}, s32[8]{0:T(128)}, u32[]{:S(2)}) copy-start(s32[8]{0:T(128)} %param.16) | copy-start | bytes 100
  234.9 23.8 %copy-start.6 = (f32[8]{0:T(128)S(1)}, f32[8]{0:T(128)}, u32[]{:S(2)}) copy-start(f32[8]{0:T(128)} %param.15) | copy-start | bytes 100
  234.9 25.4 %copy-start.4 = (bf16[1,64,18]{1,2,0:T(8,128)(2,1)S(1)}, bf16[1,64,18]{1,2,0:T(8,128)(2,1)}, u32[]{:S(2)}) copy-start(bf16[1,64,18]{1,2,0:T(8,128)(2,1)} %param.14) | copy-start | bytes 6916
  234.9 26.9 %copy-start.9 = (s32[8]{0:T(128)S(1)}, s32[8]{0:T(128)}, u32[]{:S(2)}) copy-start(s32[8]{0:T(128)} %param.17) | copy-start | bytes 100
  234.9 56.9 %copy-start.3 = (bf16[1,8,2048]{2,1,0:T(8,128)(2,1)S(1)}, bf16[1,8,2048]{2,1,0:T(8,128)(2,1)}, u32[]{:S(2)}) copy-start(bf16[1,8,2048]{2,1,0:T(8,128)(2,1)} %param.12) | copy-start | bytes 98308
  234.9 136.6 %copy-start.2 = (bf16[1,64,2048]{2,1,0:T(8,128)(2,1)S(1)}, bf16[1,64,2048]{2,1,0:T(8,128)(2,1)}, u32[]{:S(2)}) copy-start(bf16[1,64,2048]{2,1,0:T(8,128)(2,1)} %param.13) | copy-start | bytes 786436
  247.8 43.8 %all-to-all-start = ((bf16[32,8,2048]{2,1,0:T(8,128)(2,1)}), bf16[32,8,2048]{2,1,0:T(8,128)(2,1)S(1)}, u32[]{:S(2)}, u32[]{:S(2)}) async-start(bf16[32,8,2048]{2,1,0:T(8,128)(2,1)} %fusion.14), calls=%async_computation | async-start | bytes 2097152 | tf_op jit(solution)/shard_map/all_to_all | solution.py:44
  260.3 5.9 %collective-permute-start.2 = (bf16[64,18]{0,1:T(8,128)(2,1)S(1)}, bf16[64,18]{0,1:T(8,128)(2,1)S(1)}, u32[]{:S(2)}, u32[]{:S(2)}) collective-permute-start(bf16[64,18]{0,1:T(8,128)(2,1)S(1)} %fusion.23), channel_id=1, source_target_pairs={{224,0},{0,32},{32,64},{64,96},{96,128},{128,160},{160,192},{192,2... | collective-permute-start | bytes 6920 | tf_op jit(solution)/shard_map/ppermute | solution.py:51
  291.9 82.1 %collective-permute-start = (bf16[8,2048]{1,0:T(8,128)(2,1)S(1)}, bf16[8,2048]{1,0:T(8,128)(2,1)S(1)}, u32[]{:S(2)}, u32[]{:S(2)}) collective-permute-start(bf16[8,2048]{1,0:T(8,128)(2,1)S(1)} %fusion.22), channel_id=1, source_target_pairs={{224,0},{0,32},{32,64},{64,96},{96,128},{128,160},{160,192},{192,2... | collective-permute-start | bytes 98312 | tf_op jit(solution)/shard_map/ppermute | solution.py:51
  372.5 8.6 %collective-permute-start.1 = (bf16[64,2048]{1,0:T(8,128)(2,1)S(1)}, bf16[64,2048]{1,0:T(8,128)(2,1)S(1)}, u32[]{:S(2)}, u32[]{:S(2)}) collective-permute-start(bf16[64,2048]{1,0:T(8,128)(2,1)S(1)} %fusion.18), channel_id=1, source_target_pairs={{224,0},{0,32},{32,64},{64,96},{96,128},{128,160},{160,192},{192,2... | collective-permute-start | bytes 786440 | tf_op jit(solution)/shard_map/ppermute | solution.py:51
Sparse Core Ops, SparseCore 0:
  11.3 82.1 all-gather.7
  96.3 97.9 all-gather.5
  214.5 156.9 reduce-scatter.1
where the time goes:
time: 390 us; the launch traced here: 389 us
  waiting for transfers between devices  297 us (76%)
  matrix products  34.3 us (9%)
  starting transfers between devices  23.8 us (6%)
  between operations  19.1 us (5%)
  local copies, waits for them, and re-layouts  11 us (3%)
  other arithmetic  4.48 us (1%)
    all_gather x1, waiting for transfers between devices, local(): whole = lax.all_gather(own_middle, 'dp', axis=0, tiled=True)  94.4 us
    all_gather x1, waiting for transfers between devices, gather_packed(): lines, at, done = (lax.all_gather(line, axis), 0, [])  83 us
    reduce_scatter x1, waiting for transfers between devices, local(): lax.psum_scatter(contract_rows(hidden1, grad_pre2).astype(jnp.bfloat16),...  78 us
    all_to_all x2, waiting for transfers between devices, sum_at_owner(): parts = lax.all_to_all(in_blocks(shard, dim, peers), axis, 0, 0, tiled=True)  25 us
    dot_general x3, matrix products, contract_rows(): lax.dot_general(left, right, (((0,), (0,)), ((), ())), preferred_element_...  20.5 us
    all_to_all x2, starting transfers between devices, sum_at_owner(): parts = lax.all_to_all(in_blocks(shard, dim, peers), axis, 0, 0, tiled=True)  13.6 us
    dot_general x1, matrix products, local(): pre2 = jnp.dot(hidden1, whole, preferred_element_type=jnp.float32)  8.98 us
    all_to_all x1, waiting for transfers between devices, from_everyone(): lax.all_to_all(jnp.broadcast_to(shard[None], (peers, *shard.shape)), axis...  7.97 us
  transfers between devices with their start and end apart: 9, of which 7 were waited for; matrix products, arithmetic and copies ran while one was open for 7% of the time, Pallas kernels for 0%

commit v1 on v0

--- a/solution.py
+++ b/solution.py
@@ -80,7 +80,9 @@
     first, head = gather_packed((own_first, own_head), "dp", (0, 0))
     pre1 = jnp.dot(obs, first, preferred_element_type=jnp.float32)
     hidden1 = jax.nn.silu(pre1).astype(jnp.bfloat16)
-    whole = lax.all_gather(own_middle, "dp", axis=0, tiled=True)
+    whole = jnp.concatenate(
+        lax.all_to_all(jnp.stack([own_middle] * lax.axis_size("dp")), "dp", 0, 0), axis=0
+    )
     pre2 = jnp.dot(hidden1, whole, preferred_element_type=jnp.float32)
     hidden2 = jax.nn.silu(pre2).astype(jnp.bfloat16)
     squash = jnp.tanh(jnp.dot(hidden2, head, preferred_element_type=jnp.float32) / CAP)

time: 390 us -> 414 us (1.062)
  starting transfers between devices: 23.8 us -> 34.3 us
  waiting for transfers between devices: 297 us -> 306 us
    all_gather x1 -> x0, waiting for transfers between devices: 94.4 us -> none  [local(): whole = lax.all_gather(own_middle, 'dp', axis=0, tiled=True)]
    all_to_all x0 -> x1, waiting for transfers between devices: none -> 82.9 us  [local(): lax.all_to_all(jnp.stack([own_middle] * lax.axis_size('dp')), 'dp', 0, 0)]
    all_gather x1, waiting for transfers between devices: 83 us -> 104 us  [gather_packed(): lines, at, done = (lax.all_gather(line, axis), 0, [])]
    all_to_all x0 -> x1, starting transfers between devices: none -> 10.7 us  [local(): lax.all_to_all(jnp.stack([own_middle] * lax.axis_size('dp')), 'dp', 0, 0)]
    another operation x0 -> x1, local copies, waits for them, and re-layouts: none -> 5.29 us  [local(): jnp.stack([own_middle] * lax.axis_size('dp'))]
where the time goes in v1:
time: 414 us; the launch traced here: 413 us
  waiting for transfers between devices  306 us (74%)
  starting transfers between devices  34.3 us (8%)
  matrix products  34.3 us (8%)
  between operations  19.4 us (5%)
  local copies, waits for them, and re-layouts  14.8 us (4%)
  other arithmetic  4.48 us (1%)
    all_gather x1, waiting for transfers between devices, gather_packed(): lines, at, done = (lax.all_gather(line, axis), 0, [])  104 us
    all_to_all x1, waiting for transfers between devices, local(): lax.all_to_all(jnp.stack([own_middle] * lax.axis_size('dp')), 'dp', 0, 0)  82.9 us
    reduce_scatter x1, waiting for transfers between devices, local(): lax.psum_scatter(contract_rows(hidden1, grad_pre2).astype(jnp.bfloat16),...  78.6 us
    all_to_all x2, waiting for transfers between devices, sum_at_owner(): parts = lax.all_to_all(in_blocks(shard, dim, peers), axis, 0, 0, tiled=True)  24.9 us
    dot_general x3, matrix products, contract_rows(): lax.dot_general(left, right, (((0,), (0,)), ((), ())), preferred_element_...  20.5 us
    all_to_all x2, starting transfers between devices, sum_at_owner(): parts = lax.all_to_all(in_blocks(shard, dim, peers), axis, 0, 0, tiled=True)  13.8 us
    all_to_all x1, starting transfers between devices, local(): lax.all_to_all(jnp.stack([own_middle] * lax.axis_size('dp')), 'dp', 0, 0)  10.7 us
    dot_general x1, matrix products, local(): pre2 = jnp.dot(hidden1, whole, preferred_element_type=jnp.float32)  9 us
  transfers between devices with their start and end apart: 9, of which 7 were waited for; matrix products, arithmetic and copies ran while one was open for 7% of the time, Pallas kernels for 0%

profile of v1, /device:TPU:2, one launch (start us, length us, event | category | flops | bytes accessed | tf_op | source)
XLA Modules:
  0.0 413.4 jit_solution(4473134936704079647)
XLA Ops:
  7.2 0.0 copy-start
  7.2 5.3 %stack.3 = bf16[32,64,2048]{2,1,0:T(8,128)(2,1)} broadcast(bf16[64,2048]{1,0:T(8,128)(2,1)} %bitcast.82), dimensions={1,2} | broadcast | bytes 8650752 | tf_op jit(solution)/shard_map/stack | solution.py:84
  12.5 10.7 %all-to-all-start = ((bf16[32,64,2048]{2,1,0:T(8,128)(2,1)}), bf16[32,64,2048]{2,1,0:T(8,128)(2,1)}, u32[]{:S(2)}, u32[]{:S(2)}) async-start(bf16[32,64,2048]{2,1,0:T(8,128)(2,1)} %stack.3), calls=%async_computation | async-start | bytes 16777216 | tf_op jit(solution)/shard_map/all_to_all | solution.py:84
  23.2 0.0 all-gather.4.cloned.1.call-start
  23.2 0.0 copy-done.4
  23.2 0.1 copy.37
  23.3 0.1 reshape_squeeze.7
  23.5 0.0 copy-done.3
  23.5 0.7 reshape.64
  24.2 0.0 all-gather.4.cloned.1.call-update
  24.2 0.0 reduce-scatter.2.cloned.1.call-start
  24.3 104.2 %all-gather.4.cloned.1.call-done = bf16[32,1,17536]{2,1,0:T(2,128)(2,1)} async-done(((bf16[1,1,17536]{2,1,0:T(2,128)(2,1)}), bf16[32,1,17536]{2,1,0:T(2,128)(2,1)}) %all-gather.4.cloned.1.call-update) | async-done | bytes 1122320 | tf_op jit(solution)/shard_map/all_gather | solution.py:17
  128.5 1.8 copy.53
  130.2 0.1 slice.8
  130.3 0.5 reshape_reshape.6
  130.9 1.2 reshape_reshape.7
  132.1 0.0 copy-done
  132.1 2.7 fusion.11
  134.8 82.9 %all-to-all-done = bf16[32,64,2048]{2,1,0:T(8,128)(2,1)} async-done(((bf16[32,64,2048]{2,1,0:T(8,128)(2,1)}), bf16[32,64,2048]{2,1,0:T(8,128)(2,1)}, u32[]{:S(2)}, u32[]{:S(2)}) %all-to-all-start) | async-done | bytes 8388640 | tf_op jit(solution)/shard_map/all_to_all | solution.py:84
  217.8 9.0 %multiply_convert_fusion.1 = (bf16[512,2048]{0,1:T(8,128)(2,1)S(1)}, f32[512,2048]{0,1:T(8,128)S(1)}) fusion(bf16[2048,2048]{1,0:T(8,128)(2,1)} %bitcast.8, f32[2048,512]{1,0:T(8,128)} %fusion.11), kind=kOutput, calls=%fused_computation.13 | convolution fusion | flops 4305453056 | bytes 18874368 | tf_op jit(solution)/shard_map/dot_general | solution.py:86
  226.8 0.5 exponential_reduce_fusion
  227.2 0.0 copy-done.5
  227.3 0.0 copy-done.7
  227.3 0.6 multiply_reduce_fusion
  227.9 1.7 multiply_convert_fusion
  229.6 0.0 copy-start.10
  229.6 1.3 copy-done.10
  230.9 6.9 %convolution_convert_fusion = bf16[2048,2048]{1,0:T(8,128)(2,1)} fusion(bf16[512,2048]{0,1:T(8,128)(2,1)S(1)} %multiply_convert_fusion, f32[2048,512]{1,0:T(8,128)S(1)} %copy-done.1), kind=kOutput, calls=%fused_computation | convolution fusion | flops 4304404480 | bytes 14680064 | tf_op jit(solution)/shard_map/dot_general | solution.py:60
  237.8 0.0 reduce-scatter.2.cloned.1.call-update
  238.5 0.6 broadcast_in_dim.20
  239.1 4.9 %all-to-all-start.3 = ((f32[32,1,1]{2,1,0:T(1,128)}), f32[32,1,1]{2,1,0:T(1,128)S(1)}, u32[]{:S(2)}, u32[]{:S(2)}) async-start(f32[32,1,1]{2,1,0:T(1,128)} %broadcast_in_dim.20), calls=%async_computation.4 | async-start | bytes 32768 | tf_op jit(solution)/shard_map/all_to_all | solution.py:27
  244.0 0.6 convolution_convert_fusion.2
  244.6 0.2 reshape.59
  244.8 0.1 copy.54
  244.9 0.8 reshape.67
  245.7 8.0 %all-to-all-done.3 = f32[32,1,1]{2,1,0:T(1,128)S(1)} async-done(((f32[32,1,1]{2,1,0:T(1,128)}), f32[32,1,1]{2,1,0:T(1,128)S(1)}, u32[]{:S(2)}, u32[]{:S(2)}) %all-to-all-start.3) | async-done | bytes 160 | tf_op jit(solution)/shard_map/all_to_all | solution.py:27
  253.7 4.0 all-to-all-start.2
  257.7 0.0 copy-start.8
  257.7 0.0 copy-start.6
  257.7 0.0 copy-start.9
  257.7 0.0 copy-start.2
  257.8 12.9 %fusion.8 = bf16[32,8,2048]{2,1,0:T(8,128)(2,1)} fusion(f32[2048,512]{1,0:T(8,128)} %fusion.11, bf16[2048,2048]{1,0:T(8,128)(2,1)} %bitcast.8, bf16[512,2048]{0,1:T(8,128)(2,1)} %copy-done.10, bf16[1,512,256]{2,1,0:T(8,128)(2,1)S(1)} %copy-done), kind=kOutput, calls=%fused_computation.16 | convolution fusion | flops 4841799680 | bytes 15990784 | tf_op jit(solution)/shard_map/dot_general | solution.py:60
  270.7 0.0 all-to-all-done.2
  270.7 9.8 %all-to-all-start.1 = ((bf16[32,8,2048]{2,1,0:T(8,128)(2,1)}), bf16[32,8,2048]{2,1,0:T(8,128)(2,1)S(1)}, u32[]{:S(2)}, u32[]{:S(2)}) async-start(bf16[32,8,2048]{2,1,0:T(8,128)(2,1)} %fusion.8), calls=%async_computation.1 | async-start | bytes 2097152 | tf_op jit(solution)/shard_map/all_to_all | solution.py:44
  280.5 0.6 dynamic_slice.14
  281.7 0.6 fusion.19
  283.0 0.2 reshape.68
  283.2 0.1 convert_reduce_fusion.1
  283.3 1.6 collective-permute-start.2
  284.9 0.6 dynamic_slice.17
  287.4 0.6 reduce_sum.59
  288.1 1.0 collective-permute-done.2
  289.1 0.6 select_bitcast_fusion.2
  289.7 24.9 %all-to-all-done.1 = bf16[32,8,2048]{2,1,0:T(8,128)(2,1)S(1)} async-done(((bf16[32,8,2048]{2,1,0:T(8,128)(2,1)}), bf16[32,8,2048]{2,1,0:T(8,128)(2,1)S(1)}, u32[]{:S(2)}, u32[]{:S(2)}) %all-to-all-start.1) | async-done | bytes 1048608 | tf_op jit(solution)/shard_map/all_to_all | solution.py:44
  314.6 0.2 convert_reduce_fusion
  314.8 1.7 collective-permute-start
  316.5 78.6 %reduce-scatter.2.cloned.1.call-done = bf16[64,2048]{1,0:T(8,128)(2,1)} async-done(((bf16[2048,2048]{1,0:T(8,128)(2,1)}), bf16[64,2048]{1,0:T(8,128)(2,1)}) %reduce-scatter.2.cloned.1.call-update) | async-done | bytes 262160 | tf_op jit(solution)/shard_map/reduce_scatter | solution.py:101
  395.1 0.0 copy-done.2
  395.1 1.0 subtract_convert_fusion
  396.1 1.5 collective-permute-start.1
  397.6 0.0 collective-permute-done
  397.6 0.6 select_bitcast_fusion.1
  398.2 6.4 %collective-permute-done.1 = bf16[64,2048]{1,0:T(8,128)(2,1)S(1)} collective-permute-done((bf16[64,2048]{1,0:T(8,128)(2,1)S(1)}, bf16[64,2048]{1,0:T(8,128)(2,1)S(1)}, u32[]{:S(2)}, u32[]{:S(2)}) %collective-permute-start.1) | collective-permute-done | bytes 262176 | tf_op jit(solution)/shard_map/ppermute | solution.py:51
  404.7 0.7 select_bitcast_fusion
  (16 shorter events, 0.1 us)
Async XLA Ops:
  7.2 124.9 %copy-start = (bf16[1,512,256]{2,1,0:T(8,128)(2,1)S(1)}, bf16[1,512,256]{2,1,0:T(8,128)(2,1)}, u32[]{:S(2)}) copy-start(bf16[1,512,256]{2,1,0:T(8,128)(2,1)} %param.9) | copy-start | bytes 786436
  12.5 10.7 %copy-start.4 = (bf16[1,64,18]{1,2,0:T(8,128)(2,1)S(1)}, bf16[1,64,18]{1,2,0:T(8,128)(2,1)}, u32[]{:S(2)}) copy-start(bf16[1,64,18]{1,2,0:T(8,128)(2,1)} %param.14) | copy-start | bytes 6916
  12.5 11.0 %copy-start.3 = (bf16[1,8,2048]{2,1,0:T(8,128)(2,1)S(1)}, bf16[1,8,2048]{2,1,0:T(8,128)(2,1)}, u32[]{:S(2)}) copy-start(bf16[1,8,2048]{2,1,0:T(8,128)(2,1)} %param.12) | copy-start | bytes 98308
  12.5 205.3 %all-to-all-start = ((bf16[32,64,2048]{2,1,0:T(8,128)(2,1)}), bf16[32,64,2048]{2,1,0:T(8,128)(2,1)}, u32[]{:S(2)}, u32[]{:S(2)}) async-start(bf16[32,64,2048]{2,1,0:T(8,128)(2,1)} %stack.3), calls=%async_computation | async-start | bytes 16777216 | tf_op jit(solution)/shard_map/all_to_all | solution.py:84
  23.2 105.3 %all-gather.4.cloned.1.call-start = ((), (), s32[]{:S(2)}) async-start(), calls=%async_computation.6 | async-start | bytes 2314752 | tf_op jit(solution)/shard_map/all_gather | solution.py:17
  24.2 370.9 %reduce-scatter.2.cloned.1.call-start = ((), (), s32[]{:S(2)}) async-start(), calls=%async_computation.5 | async-start | bytes 8650752 | tf_op jit(solution)/shard_map/reduce_scatter | solution.py:101
  217.8 9.5 %copy-start.5 = (s32[1,512]{1,0:T(1,128)S(1)}, s32[1,512]{1,0:T(1,128)}, u32[]{:S(2)}) copy-start(s32[1,512]{1,0:T(1,128)} %param.11) | copy-start | bytes 6148
  217.8 9.5 %copy-start.7 = (f32[1,512]{1,0:T(1,128)S(1)}, f32[1,512]{1,0:T(1,128)}, u32[]{:S(2)}) copy-start(f32[1,512]{1,0:T(1,128)} %param.10) | copy-start | bytes 6148
  227.9 3.0 copy-start.1
  229.6 1.3 copy-start.10
  239.1 14.5 %all-to-all-start.3 = ((f32[32,1,1]{2,1,0:T(1,128)}), f32[32,1,1]{2,1,0:T(1,128)S(1)}, u32[]{:S(2)}, u32[]{:S(2)}) async-start(f32[32,1,1]{2,1,0:T(1,128)} %broadcast_in_dim.20), calls=%async_computation.4 | async-start | bytes 32768 | tf_op jit(solution)/shard_map/all_to_all | solution.py:27
  253.7 17.0 %all-to-all-start.2 = ((bf16[32,2,576]{2,1,0:T(2,128)(2,1)}), bf16[32,2,576]{2,1,0:T(2,128)(2,1)S(1)}, u32[]{:S(2)}, u32[]{:S(2)}) async-start(bf16[32,2,576]{2,1,0:T(2,128)(2,1)} %reshape.67), calls=%async_computation.3 | async-start | bytes 163840 | tf_op jit(solution)/shard_map/all_to_all | solution.py:44
  257.7 22.8 %copy-start.8 = (s32[8]{0:T(128)S(1)}, s32[8]{0:T(128)}, u32[]{:S(2)}) copy-start(s32[8]{0:T(128)} %param.16) | copy-start | bytes 100
  257.7 24.0 %copy-start.6 = (f32[8]{0:T(128)S(1)}, f32[8]{0:T(128)}, u32[]{:S(2)}) copy-start(f32[8]{0:T(128)} %param.15) | copy-start | bytes 100
  257.7 27.2 %copy-start.9 = (s32[8]{0:T(128)S(1)}, s32[8]{0:T(128)}, u32[]{:S(2)}) copy-start(s32[8]{0:T(128)} %param.17) | copy-start | bytes 100
  257.7 137.3 %copy-start.2 = (bf16[1,64,2048]{2,1,0:T(8,128)(2,1)S(1)}, bf16[1,64,2048]{2,1,0:T(8,128)(2,1)}, u32[]{:S(2)}) copy-start(bf16[1,64,2048]{2,1,0:T(8,128)(2,1)} %param.13) | copy-start | bytes 786436
  270.7 44.0 %all-to-all-start.1 = ((bf16[32,8,2048]{2,1,0:T(8,128)(2,1)}), bf16[32,8,2048]{2,1,0:T(8,128)(2,1)S(1)}, u32[]{:S(2)}, u32[]{:S(2)}) async-start(bf16[32,8,2048]{2,1,0:T(8,128)(2,1)} %fusion.8), calls=%async_computation.1 | async-start | bytes 2097152 | tf_op jit(solution)/shard_map/all_to_all | solution.py:44
  283.3 5.8 %collective-permute-start.2 = (bf16[64,18]{0,1:T(8,128)(2,1)S(1)}, bf16[64,18]{0,1:T(8,128)(2,1)S(1)}, u32[]{:S(2)}, u32[]{:S(2)}) collective-permute-start(bf16[64,18]{0,1:T(8,128)(2,1)S(1)} %fusion.14), channel_id=1, source_target_pairs={{224,0},{0,32},{32,64},{64,96},{96,128},{128,160},{160,192},{192,2... | collective-permute-start | bytes 6920 | tf_op jit(solution)/shard_map/ppermute | solution.py:51
  314.8 82.8 %collective-permute-start = (bf16[8,2048]{1,0:T(8,128)(2,1)S(1)}, bf16[8,2048]{1,0:T(8,128)(2,1)S(1)}, u32[]{:S(2)}, u32[]{:S(2)}) collective-permute-start(bf16[8,2048]{1,0:T(8,128)(2,1)S(1)} %fusion.13), channel_id=1, source_target_pairs={{224,0},{0,32},{32,64},{64,96},{96,128},{128,160},{160,192},{192,2... | collective-permute-start | bytes 98312 | tf_op jit(solution)/shard_map/ppermute | solution.py:51
  396.1 8.6 %collective-permute-start.1 = (bf16[64,2048]{1,0:T(8,128)(2,1)S(1)}, bf16[64,2048]{1,0:T(8,128)(2,1)S(1)}, u32[]{:S(2)}, u32[]{:S(2)}) collective-permute-start(bf16[64,2048]{1,0:T(8,128)(2,1)S(1)} %subtract_convert_fusion), channel_id=1, source_target_pairs={{224,0},{0,32},{32,64},{64,96},{96,128},{128,160},{160,192},{192,2... | collective-permute-start | bytes 786440 | tf_op jit(solution)/shard_map/ppermute | solution.py:51
Sparse Core Ops, SparseCore 0:
  27.3 101.1 all-gather.3
  238.0 157.0 reduce-scatter.1
